TPU v7x, 32 devices: a whole 2x2x4 slice. The times are simulated.
32 devices in a mesh: shard: 4 (over y, x), seq: 8 (over z, core).
Axes of the slice: x: 2, y: 2, z: 4, core: 2. Of those that a mesh axis runs over, the one named last changes fastest.
Arguments:
- inputs: bfloat16 [4, 1024, 2048], P('shard', 'seq'), may hold values from -6 to 6
- attn_gain: bfloat16 [2048], P(('shard', 'seq')), may hold values from 0.25 to 1.75
- query_project_weight: bfloat16 [2048, 3072], P('shard', 'seq'), may hold values from -0.25 to 0.25
- latent_project_weight: bfloat16 [2048, 576], P(('shard', 'seq')), may hold values from -0.125 to 0.125
- latent_gain: bfloat16 [512], P(('shard', 'seq')), may hold values from 0.25 to 1.75
- latent_keyval_weight: bfloat16 [512, 4096], P('shard', 'seq'), may hold values from -0.25 to 0.25
- attention_output_weight: bfloat16 [2048, 2048], P('seq', 'shard'), may hold values from -0.5 to 0.5
- ffn_gain: bfloat16 [2048], P(('shard', 'seq')), may hold values from 0.25 to 1.75
- shared_gate: bfloat16 [2048, 2816], P('shard', 'seq'), may hold values from -0.125 to 0.125
- shared_up: bfloat16 [2048, 2816], P('shard', 'seq'), may hold values from -0.125 to 0.125
- shared_down: bfloat16 [2816, 2048], P('seq', 'shard'), may hold values from -0.109375 to 0.109375
- expert_gate: bfloat16 [8, 2048, 1408], P('seq', 'shard'), may hold values from -0.125 to 0.125
- expert_up: bfloat16 [8, 2048, 1408], P('seq', 'shard'), may hold values from -0.125 to 0.125
- expert_down: bfloat16 [8, 1408, 2048], P('seq', None, 'shard'), may hold values from -0.15625 to 0.15625
- routes: int32 [4, 1024, 6], P('shard', 'seq'), may hold values from 0 to 7, as said below
- slots: int32 [4, 1024, 6], P('shard', 'seq'), may hold values from 0 to 108, as said below
- gates: bfloat16 [4, 1024, 6], P('shard', 'seq'), may hold values from 0.099609375 to 0.5
- cotangent: bfloat16 [4, 1024, 2048], P('shard', 'seq'), may hold values from -6 to 6
Outputs:
- output: bfloat16 [4, 1024, 2048], P('shard', 'seq')
- input_grad: float32 [4, 1024, 2048], P('shard', 'seq')
- attn_gain_grad: float32 [2048], P(('shard', 'seq'))
- query_grad: float32 [2048, 3072], P('shard', 'seq')
- latent_grad: float32 [2048, 576], P(('shard', 'seq'))
- latent_gain_grad: float32 [512], P(('shard', 'seq'))
- kvup_grad: float32 [512, 4096], P('shard', 'seq')
- out_grad: float32 [2048, 2048], P('seq', 'shard')
- ffn_gain_grad: float32 [2048], P(('shard', 'seq'))
- shared_gate_grad: float32 [2048, 2816], P('shard', 'seq')
- shared_up_grad: float32 [2048, 2816], P('shard', 'seq')
- shared_down_grad: float32 [2816, 2048], P('seq', 'shard')
- expert_gate_grad: float32 [8, 2048, 1408], P('seq', 'shard')
- expert_up_grad: float32 [8, 2048, 1408], P('seq', 'shard')
- expert_down_grad: float32 [8, 1408, 2048], P('seq', None, 'shard')
Inputs may be any that keep to these rules, and one draw needn't show every extreme that they name: `routes`: each token names 6 different experts. In each device's block of 128 tokens one expert is named by more than 108 tokens. `slots`: within each device's block of 128 tokens, the routes to one expert carry the numbers 0, 1, 2 and so on, each once, in an order drawn from the seed, except that every number from 108 on is written as 108; such routes are dropped.
All inputs are finite; a program needn't handle non-finite values.
Results may differ from a plain program's by a relative error of at most 0.025.
Values may be sent and summed in bfloat16 or wider, within the bound.
A program may use at most 256 MiB of HBM per device.

v0:
```python
import jax
import jax.numpy as jnp
from jax import lax
from jax.sharding import PartitionSpec as P

HEADS = 16
NOPE = 128
ROPE = 64
VDIM = 128
RANK = 512
TOPK = 6
EXP_DEV = 1


EPSILON = 1e-06
THETA = 10000.0
MASKED = -1e30


def rope_tables(positions, depth):
    half_depth = depth // 2
    frequency = THETA ** (-(2.0 * jnp.arange(half_depth, dtype=jnp.float32)) / depth)
    angles = positions.astype(jnp.float32)[:, None] * frequency[None, :]
    return (jnp.cos(angles), jnp.sin(angles))


def rotate(values, cosine, sine):
    half_depth = values.shape[-1] // 2
    first = values[..., :half_depth]
    second = values[..., half_depth:]
    return jnp.concatenate([first * cosine - second * sine, second * cosine + first * sine], -1)


def norm_forward(values, scaling):
    inverse = lax.rsqrt(jnp.mean(values * values, -1, keepdims=True) + EPSILON)
    return (values * inverse * scaling, inverse)


def norm_backward(values, inverse, scaling, upstream):
    weighted = upstream * scaling
    scaling_grad = jnp.sum(upstream * values * inverse, 0)
    centre = jnp.mean(weighted * values, -1, keepdims=True)
    return (inverse * weighted - values * inverse**3 * centre, scaling_grad)


def swish_gradient(gate_pre, upper, upstream):
    sigma = jax.nn.sigmoid(gate_pre)
    return (
        upstream * upper * sigma * (1.0 + gate_pre * (1.0 - sigma)),
        upstream * gate_pre * sigma,
    )


def inner_rows(left, right):
    return lax.dot_general(
        left, right, (((0,), (0,)), ((), ())), preferred_element_type=jnp.float32
    )


def times_transposed(left, right):
    return lax.dot_general(
        left, right, (((1,), (1,)), ((), ())), preferred_element_type=jnp.float32
    )


def masked_scores(queries, keys, offset, score_scale):
    scores = (
        jnp.einsum("qhd,khd->hqk", queries, keys, preferred_element_type=jnp.float32) * score_scale
    )
    query_pos = offset + jnp.arange(queries.shape[0])
    seen = jnp.arange(keys.shape[0])[None, :] <= query_pos[:, None]
    return jnp.where(seen[None], scores, MASKED)


def to_experts(buffer):
    return lax.all_to_all(buffer, "seq", split_axis=0, concat_axis=1, tiled=True)


def to_sources(buffer):
    return lax.all_to_all(buffer, "seq", split_axis=1, concat_axis=0, tiled=True)


def expert_forward_pass(
    arrived_rows, complete_expert_gate, complete_expert_up, complete_expert_down
):
    expert_gate_input = jnp.einsum(
        "zni,ziv->znv", arrived_rows, complete_expert_gate, preferred_element_type=jnp.float32
    )
    expert_up_input = jnp.einsum(
        "zni,ziv->znv", arrived_rows, complete_expert_up, preferred_element_type=jnp.float32
    )
    expert_hidden_rows = (jax.nn.silu(expert_gate_input) * expert_up_input).astype(jnp.bfloat16)
    expert_output_rows = jnp.einsum(
        "erf,efd->erd", expert_hidden_rows, complete_expert_down, preferred_element_type=jnp.float32
    ).astype(jnp.bfloat16)
    return (expert_gate_input, expert_up_input, expert_hidden_rows, expert_output_rows)


def on_device(
    inputs,
    attn_gain,
    query_project_weight,
    latent_project_weight,
    latent_gain,
    latent_keyval_weight,
    attention_output_weight,
    ffn_gain,
    shared_gate,
    shared_up,
    shared_down,
    expert_gate,
    expert_up,
    expert_down,
    routes,
    slots,
    gates,
    cotangent,
):
    tok_rows = inputs.shape[1]
    model_width = inputs.shape[2]
    groups = lax.axis_size("seq")
    local_heads = HEADS // groups
    query_width = NOPE + ROPE
    experts = EXP_DEV * groups
    capacity = 9 * tok_rows * TOPK // (8 * experts)
    length = tok_rows * groups
    score_scale = (NOPE + ROPE) ** (-0.5)
    block_rows = min(512, length)
    starts = jnp.arange(length // block_rows) * block_rows
    first_norm_weight, full_latent, latent_norm_weight, second_norm_weight = (
        lax.all_gather(attn_gain, ("shard", "seq"), axis=0, tiled=True),
        lax.all_gather(latent_project_weight, ("shard", "seq"), axis=0, tiled=True),
        lax.all_gather(latent_gain, ("shard", "seq"), axis=0, tiled=True),
        lax.all_gather(ffn_gain, ("shard", "seq"), axis=0, tiled=True),
    )
    first_norm_weight = first_norm_weight.astype(jnp.float32)
    latent_norm_weight = latent_norm_weight.astype(jnp.float32)
    second_norm_weight = second_norm_weight.astype(jnp.float32)
    column_weights = (
        lax.all_gather(query_project_weight, "shard", axis=0, tiled=True),
        lax.all_gather(latent_keyval_weight, "shard", axis=0, tiled=True),
        lax.all_gather(attention_output_weight, "shard", axis=1, tiled=True),
        lax.all_gather(shared_gate, "shard", axis=0, tiled=True),
        lax.all_gather(shared_up, "shard", axis=0, tiled=True),
        lax.all_gather(shared_down, "shard", axis=1, tiled=True),
        lax.all_gather(expert_gate, "shard", axis=1, tiled=True),
        lax.all_gather(expert_up, "shard", axis=1, tiled=True),
        lax.all_gather(expert_down, "shard", axis=2, tiled=True),
    )
    (
        full_query,
        full_kvup,
        full_out,
        full_sgate,
        full_sup,
        full_sdown,
        complete_expert_gate,
        complete_expert_up,
        complete_expert_down,
    ) = column_weights
    residual_stream = inputs.reshape(tok_rows, model_width).astype(jnp.float32)
    normed, inv_one = norm_forward(residual_stream, first_norm_weight)
    first = normed.astype(jnp.bfloat16)
    positions = lax.axis_index("seq") * tok_rows + jnp.arange(tok_rows)
    cos_local, sin_local = rope_tables(positions, ROPE)
    latent = jnp.dot(first, full_latent, preferred_element_type=jnp.float32)
    compressed = latent[:, :RANK]
    latent_normed, inv_latent = norm_forward(compressed, latent_norm_weight)
    latent_low = latent_normed.astype(jnp.bfloat16)
    key_rope = rotate(latent[:, RANK:], cos_local, sin_local).astype(jnp.bfloat16)
    first_all, latent_all, rope_all = (
        lax.all_gather(first, "seq", axis=0, tiled=True),
        lax.all_gather(latent_low, "seq", axis=0, tiled=True),
        lax.all_gather(key_rope, "seq", axis=0, tiled=True),
    )
    cos_all, sin_all = rope_tables(jnp.arange(length), ROPE)
    head_query = jnp.dot(first_all, full_query, preferred_element_type=jnp.float32).reshape(
        length, local_heads, query_width
    )
    head_query = jnp.concatenate(
        [
            head_query[..., :NOPE],
            rotate(head_query[..., NOPE:], cos_all[:, None], sin_all[:, None]),
        ],
        -1,
    ).astype(jnp.bfloat16)
    keyval = (
        jnp.dot(latent_all, full_kvup, preferred_element_type=jnp.float32)
        .astype(jnp.bfloat16)
        .reshape(length, local_heads, NOPE + VDIM)
    )
    head_keys = jnp.concatenate(
        [keyval[..., :NOPE], jnp.broadcast_to(rope_all[:, None, :], (length, local_heads, ROPE))],
        -1,
    )
    head_values = keyval[..., NOPE:]

    def forward_block(offset):
        queries = lax.dynamic_slice_in_dim(head_query, offset, block_rows, 0)
        scores = masked_scores(queries, head_keys, offset, score_scale)
        top = jnp.max(scores, -1, keepdims=True)
        expo = jnp.exp(scores - top)
        total = jnp.sum(expo, -1, keepdims=True)
        probs_low = (expo / total).astype(jnp.bfloat16)
        result = jnp.einsum(
            "hqk,khd->qhd", probs_low, head_values, preferred_element_type=jnp.float32
        ).astype(jnp.bfloat16)
        return (result, (top + jnp.log(total))[..., 0])

    attended_blocks, log_totals = lax.map(forward_block, starts)
    attended = attended_blocks.reshape(length, local_heads * VDIM)
    middle = residual_stream + lax.psum_scatter(
        jnp.dot(attended, full_out, preferred_element_type=jnp.float32).astype(jnp.bfloat16),
        "seq",
        scatter_dimension=0,
        tiled=True,
    ).astype(jnp.float32)
    normed_two, inv_two = norm_forward(middle, second_norm_weight)
    second = normed_two.astype(jnp.bfloat16)
    upstream = cotangent.reshape(tok_rows, model_width)
    second_all, upstream_all = (
        lax.all_gather(second, "seq", axis=0, tiled=True),
        lax.all_gather(upstream, "seq", axis=0, tiled=True),
    )
    sgate_pre = jnp.dot(second_all, full_sgate, preferred_element_type=jnp.float32)
    sup_pre = jnp.dot(second_all, full_sup, preferred_element_type=jnp.float32)
    shidden = (jax.nn.silu(sgate_pre) * sup_pre).astype(jnp.bfloat16)
    shared_out = lax.psum_scatter(
        jnp.dot(shidden, full_sdown, preferred_element_type=jnp.float32).astype(jnp.bfloat16),
        "seq",
        scatter_dimension=0,
        tiled=True,
    ).astype(jnp.float32)
    route_rows = routes.reshape(tok_rows, TOPK)
    slot_rows = slots.reshape(tok_rows, TOPK)
    slot_ids = jnp.where(slot_rows < capacity, route_rows * capacity + slot_rows, -1)
    columns = jnp.arange(experts * capacity)
    match = slot_ids[:, :, None] == columns[None, None, :]
    picks = jnp.any(match, 1).astype(jnp.bfloat16)
    gate_table = jnp.sum(
        jnp.where(match, gates.reshape(tok_rows, TOPK).astype(jnp.float32)[:, :, None], 0.0), 1
    ).astype(jnp.bfloat16)
    dispatched = (
        inner_rows(picks, second).astype(jnp.bfloat16).reshape(experts, capacity, model_width)
    )
    arrived_rows = to_experts(dispatched)
    expert_gate_input, expert_up_input, expert_hidden_rows, expert_output_rows = (
        expert_forward_pass(
            arrived_rows, complete_expert_gate, complete_expert_up, complete_expert_down
        )
    )
    returned = to_sources(expert_output_rows).reshape(experts * capacity, model_width)
    routed = jnp.dot(gate_table, returned, preferred_element_type=jnp.float32)
    output = (middle + shared_out + routed).astype(jnp.bfloat16).reshape(1, tok_rows, model_width)
    column_back = (
        lax.all_gather(query_project_weight, "shard", axis=0, tiled=True),
        lax.all_gather(latent_keyval_weight, "shard", axis=0, tiled=True),
        lax.all_gather(attention_output_weight, "shard", axis=1, tiled=True),
        lax.all_gather(shared_gate, "shard", axis=0, tiled=True),
        lax.all_gather(shared_up, "shard", axis=0, tiled=True),
        lax.all_gather(shared_down, "shard", axis=1, tiled=True),
        lax.all_gather(expert_gate, "shard", axis=1, tiled=True),
        lax.all_gather(expert_up, "shard", axis=1, tiled=True),
        lax.all_gather(expert_down, "shard", axis=2, tiled=True),
    )
    (
        full_query,
        full_kvup,
        full_out,
        full_sgate,
        full_sup,
        full_sdown,
        complete_expert_gate,
        complete_expert_up,
        complete_expert_down,
    ) = column_back
    upstream_full = upstream.astype(jnp.float32)
    d_sdown = inner_rows(shidden, upstream_all)
    d_shidden = times_transposed(upstream_all, full_sdown)
    d_sgate, d_sup = swish_gradient(sgate_pre, sup_pre, d_shidden)
    d_sgate = d_sgate.astype(jnp.bfloat16)
    d_sup = d_sup.astype(jnp.bfloat16)
    d_wsgate = inner_rows(second_all, d_sgate)
    d_wsup = inner_rows(second_all, d_sup)
    d_second = lax.psum_scatter(
        (times_transposed(d_sgate, full_sgate) + times_transposed(d_sup, full_sup)).astype(
            jnp.bfloat16
        ),
        "seq",
        scatter_dimension=0,
        tiled=True,
    ).astype(jnp.float32)
    d_eoutput = (
        inner_rows(gate_table, upstream)
        .astype(jnp.bfloat16)
        .reshape(experts, capacity, model_width)
    )
    d_received_out = to_experts(d_eoutput)
    d_edown = jnp.einsum(
        "erf,erd->efd", expert_hidden_rows, d_received_out, preferred_element_type=jnp.float32
    )
    expert_hidden_grad_rows = jnp.einsum(
        "erd,efd->erf", d_received_out, complete_expert_down, preferred_element_type=jnp.float32
    )
    expert_gate_input_grad, expert_up_input_grad = swish_gradient(
        expert_gate_input, expert_up_input, expert_hidden_grad_rows
    )
    expert_gate_input_grad = expert_gate_input_grad.astype(jnp.bfloat16)
    expert_up_input_grad = expert_up_input_grad.astype(jnp.bfloat16)
    d_egate = jnp.einsum(
        "gyh,gya->gha", arrived_rows, expert_gate_input_grad, preferred_element_type=jnp.float32
    )
    expert_up_output_grad = jnp.einsum(
        "gyh,gya->gha", arrived_rows, expert_up_input_grad, preferred_element_type=jnp.float32
    )
    d_slots = (
        jnp.einsum(
            "ams,aus->amu",
            expert_gate_input_grad,
            complete_expert_gate,
            preferred_element_type=jnp.float32,
        )
        + jnp.einsum(
            "ams,aus->amu",
            expert_up_input_grad,
            complete_expert_up,
            preferred_element_type=jnp.float32,
        )
    ).astype(jnp.bfloat16)
    d_back = to_sources(d_slots).reshape(experts * capacity, model_width)
    d_second = d_second + jnp.dot(picks, d_back, preferred_element_type=jnp.float32)
    d_middle_norm, d_gain_two = norm_backward(middle, inv_two, second_norm_weight, d_second)
    d_middle = upstream_full + d_middle_norm
    d_branch = d_middle.astype(jnp.bfloat16)
    d_branch_all = lax.all_gather(d_branch, "seq", axis=0, tiled=True)
    d_wout = inner_rows(attended, d_branch_all)
    d_heads = (
        times_transposed(d_branch_all, full_out)
        .astype(jnp.bfloat16)
        .reshape(length, local_heads, VDIM)
    )

    def backward_block(carry, element):
        offset, block_lse = element
        key_sum, value_sum = carry
        queries = lax.dynamic_slice_in_dim(head_query, offset, block_rows, 0)
        d_out = lax.dynamic_slice_in_dim(d_heads, offset, block_rows, 0)
        scores = masked_scores(queries, head_keys, offset, score_scale)
        probs = jnp.exp(scores - block_lse[..., None])
        probs_low = probs.astype(jnp.bfloat16)
        d_probs = jnp.einsum("qhd,khd->hqk", d_out, head_values, preferred_element_type=jnp.float32)
        centre = jnp.sum(probs * d_probs, -1, keepdims=True)
        d_scores = (probs * (d_probs - centre)).astype(jnp.bfloat16)
        d_queries = (
            jnp.einsum("hqk,khd->qhd", d_scores, head_keys, preferred_element_type=jnp.float32)
            * score_scale
        )
        key_sum = (
            key_sum
            + jnp.einsum("hqk,qhd->khd", d_scores, queries, preferred_element_type=jnp.float32)
            * score_scale
        )
        value_sum = value_sum + jnp.einsum(
            "hqk,qhd->khd", probs_low, d_out, preferred_element_type=jnp.float32
        )
        return ((key_sum, value_sum), d_queries)

    zero_keys = jnp.zeros((length, local_heads, query_width), jnp.float32)
    zero_values = jnp.zeros((length, local_heads, VDIM), jnp.float32)
    (d_keys, d_values), d_queries = lax.scan(
        backward_block, (zero_keys, zero_values), (starts, log_totals)
    )
    d_queries = d_queries.reshape(length, local_heads, query_width)
    d_queries = jnp.concatenate(
        [d_queries[..., :NOPE], rotate(d_queries[..., NOPE:], cos_all[:, None], -sin_all[:, None])],
        -1,
    )
    d_queries = d_queries.astype(jnp.bfloat16).reshape(length, local_heads * query_width)
    d_keys = d_keys.astype(jnp.bfloat16)
    d_values = d_values.astype(jnp.bfloat16)
    d_keyval = jnp.concatenate([d_keys[..., :NOPE], d_values], -1).reshape(
        length, local_heads * (NOPE + VDIM)
    )
    d_wkvup = inner_rows(latent_all, d_keyval)
    d_wquery = inner_rows(first_all, d_queries)
    first_part = times_transposed(d_queries, full_query)
    latent_part = times_transposed(d_keyval, full_kvup)
    rope_part = jnp.sum(d_keys[..., NOPE:].astype(jnp.float32), 1)
    first_back, latent_back, rope_back = (
        lax.psum_scatter(
            first_part.astype(jnp.bfloat16), "seq", scatter_dimension=0, tiled=True
        ).astype(jnp.float32),
        lax.psum_scatter(
            latent_part.astype(jnp.bfloat16), "seq", scatter_dimension=0, tiled=True
        ).astype(jnp.float32),
        lax.psum_scatter(
            rope_part.astype(jnp.bfloat16), "seq", scatter_dimension=0, tiled=True
        ).astype(jnp.float32),
    )
    d_rope = rotate(rope_back, cos_local, -sin_local)
    d_compressed, d_gain_latent = norm_backward(
        compressed, inv_latent, latent_norm_weight, latent_back
    )
    d_latent = jnp.concatenate([d_compressed, d_rope], -1).astype(jnp.bfloat16)
    d_wlatent = inner_rows(first, d_latent)
    d_first = first_back + times_transposed(d_latent, full_latent)
    d_resid, d_gain_one = norm_backward(residual_stream, inv_one, first_norm_weight, d_first)
    input_grad = (d_middle + d_resid).reshape(1, tok_rows, model_width)
    shard_sums = (
        lax.psum_scatter(
            d_wquery.astype(jnp.bfloat16), "shard", scatter_dimension=0, tiled=True
        ).astype(jnp.float32),
        lax.psum_scatter(
            d_wkvup.astype(jnp.bfloat16), "shard", scatter_dimension=0, tiled=True
        ).astype(jnp.float32),
        lax.psum_scatter(
            d_wout.astype(jnp.bfloat16), "shard", scatter_dimension=1, tiled=True
        ).astype(jnp.float32),
        lax.psum_scatter(
            d_wsgate.astype(jnp.bfloat16), "shard", scatter_dimension=0, tiled=True
        ).astype(jnp.float32),
        lax.psum_scatter(
            d_wsup.astype(jnp.bfloat16), "shard", scatter_dimension=0, tiled=True
        ).astype(jnp.float32),
        lax.psum_scatter(
            d_sdown.astype(jnp.bfloat16), "shard", scatter_dimension=1, tiled=True
        ).astype(jnp.float32),
        lax.psum_scatter(
            d_egate.astype(jnp.bfloat16), "shard", scatter_dimension=1, tiled=True
        ).astype(jnp.float32),
        lax.psum_scatter(
            expert_up_output_grad.astype(jnp.bfloat16), "shard", scatter_dimension=1, tiled=True
        ).astype(jnp.float32),
        lax.psum_scatter(
            d_edown.astype(jnp.bfloat16), "shard", scatter_dimension=2, tiled=True
        ).astype(jnp.float32),
    )
    (
        query_grad,
        kvup_grad,
        out_grad,
        shared_gate_grad,
        shared_up_grad,
        shared_down_grad,
        expert_gate_grad,
        expert_up_grad,
        expert_down_grad,
    ) = shard_sums
    attn_gain_grad, latent_grad, latent_gain_grad, ffn_gain_grad = (
        lax.psum_scatter(d_gain_one, ("shard", "seq"), scatter_dimension=0, tiled=True),
        lax.psum_scatter(d_wlatent, ("shard", "seq"), scatter_dimension=0, tiled=True),
        lax.psum_scatter(d_gain_latent, ("shard", "seq"), scatter_dimension=0, tiled=True),
        lax.psum_scatter(d_gain_two, ("shard", "seq"), scatter_dimension=0, tiled=True),
    )
    return (
        output,
        input_grad,
        attn_gain_grad,
        query_grad,
        latent_grad,
        latent_gain_grad,
        kvup_grad,
        out_grad,
        ffn_gain_grad,
        shared_gate_grad,
        shared_up_grad,
        shared_down_grad,
        expert_gate_grad,
        expert_up_grad,
        expert_down_grad,
    )


def solution(mesh):
    in_specs = (
        P("shard", "seq", None),
        P(("shard", "seq")),
        P("shard", "seq"),
        P(("shard", "seq"), None),
        P(("shard", "seq")),
        P("shard", "seq"),
        P("seq", "shard"),
        P(("shard", "seq")),
        P("shard", "seq"),
        P("shard", "seq"),
        P("seq", "shard"),
        P("seq", "shard", None),
        P("seq", "shard", None),
        P("seq", None, "shard"),
        P("shard", "seq", None),
        P("shard", "seq", None),
        P("shard", "seq", None),
        P("shard", "seq", None),
    )
    out_specs = (
        P("shard", "seq", None),
        P("shard", "seq", None),
        P(("shard", "seq")),
        P("shard", "seq"),
        P(("shard", "seq"), None),
        P(("shard", "seq")),
        P("shard", "seq"),
        P("seq", "shard"),
        P(("shard", "seq")),
        P("shard", "seq"),
        P("shard", "seq"),
        P("seq", "shard"),
        P("seq", "shard", None),
        P("seq", "shard", None),
        P("seq", None, "shard"),
    )
    return jax.shard_map(
        on_device, mesh=mesh, in_specs=in_specs, out_specs=out_specs, check_vma=False
    )
```

profile of v0, /device:TPU:0, one launch (start us, length us, event | category | flops | bytes accessed | tf_op | source)
XLA Modules:
  0.0 1747.2 jit_solution(12330881947437891462)
XLA Ops:
  10.6 42.3 %all-reduce.7 = (bf16[2048]{0:T(1024)(128)(2,1)S(1)}, bf16[512]{0:T(512)(128)(2,1)S(1)}, bf16[2048]{0:T(1024)(128)(2,1)S(1)}) all-reduce(bf16[2048]{0:T(1024)(128)(2,1)S(1)} %dynamic-update-slice, bf16[512]{0:T(512)(128)(2,1)S(1)} %dynamic-update-slice.1, ...), channel_id=1, replica_groups=mesh['shard'=4,'seq'=8] {'shard','seq'}, use_global_device_ids=true, to_apply=%add | all-reduce | flops 4608 | bytes 18432
  56.0 15.4 all-gather.20.cloned.1.call-done
  105.8 24.3 %all-gather.18.cloned.1.call-done = bf16[2048,384]{1,0:T(8,128)(2,1)} async-done(((bf16[512,384]{1,0:T(8,128)(2,1)}), bf16[2048,384]{1,0:T(8,128)(2,1)}) %all-gather.18.cloned.1.call-update) | async-done | bytes 1572880 | tf_op jit(solution)/shard_map/all_gather | solution.py:140
  130.1 48.9 %all-gather.16.cloned.1.call-done = bf16[1024,2048]{1,0:T(8,128)(2,1)} async-done(((bf16[128,2048]{1,0:T(8,128)(2,1)}), bf16[1024,2048]{1,0:T(8,128)(2,1)}) %all-gather.16.cloned.1.call-update) | async-done | bytes 4194320 | tf_op jit(solution)/shard_map/all_gather | solution.py:172
  184.6 20.3 %while.27 = (s32[]{:T(128)}, bf16[2,512,2,128]{3,2,1,0:T(2,128)(2,1)S(1)}, f32[2,2,512]{2,1,0:T(2,128)S(1)}, s32[2]{0:T(128)S(1)}, bf16[1024,2,192]{0,2,1:T(8,12...) while((s32[]{:T(128)}, ...), condition=%wide.region_5.6_spmd, body=%wide.region_2.5_spmd.sunk | while | flops 684326400 | bytes 17207468 | solution.py:210
  213.3 47.1 %reduce-scatter.21.cloned.1.call-done = bf16[128,2048]{1,0:T(8,128)(2,1)} async-done(((bf16[1024,2048]{1,0:T(8,128)(2,1)}), bf16[128,2048]{1,0:T(8,128)(2,1)}) %reduce-scatter.21.cloned.1.call-update) | async-done | bytes 524304 | tf_op jit(solution)/shard_map/reduce_scatter | solution.py:212
  285.3 74.2 %all-to-all-done.2 = bf16[8,108,2048]{2,1,0:T(8,128)(2,1)} async-done(((bf16[8,108,2048]{2,1,0:T(8,128)(2,1)}), bf16[8,108,2048]{2,1,0:T(8,128)(2,1)}, u32[]{:S(2)}, u32[]{:S(2)}) %all-to-all-start.2) | async-done | bytes 3538976 | tf_op jit(solution)/shard_map/all_to_all | solution.py:76
  380.6 66.2 %all-to-all-done = bf16[8,108,2048]{2,1,0:T(8,128)(2,1)} async-done(((bf16[8,108,2048]{2,1,0:T(8,128)(2,1)}), bf16[8,108,2048]{2,1,0:T(8,128)(2,1)}, u32[]{:S(2)}, u32[]{:S(2)}) %all-to-all-start) | async-done | bytes 3538976 | tf_op jit(solution)/shard_map/all_to_all | solution.py:76
  461.9 14.9 multiply_convert_fusion.2
  476.8 16.0 all-gather.28.cloned.1.call-done
  492.7 49.1 %all-gather.26.cloned.1.call-done = bf16[1024,2048]{1,0:T(8,128)(2,1)} async-done(((bf16[128,2048]{1,0:T(8,128)(2,1)}), bf16[1024,2048]{1,0:T(8,128)(2,1)}) %all-gather.26.cloned.1.call-update) | async-done | bytes 4194320 | tf_op jit(solution)/shard_map/all_gather | solution.py:222
  547.2 24.7 %all-gather.30.cloned.1.call-done = bf16[2048,352]{0,1:T(8,128)(2,1)} async-done(((bf16[512,352]{0,1:T(8,128)(2,1)}), bf16[2048,352]{0,1:T(8,128)(2,1)}) %all-gather.30.cloned.1.call-update) | async-done | bytes 1441808 | tf_op jit(solution)/shard_map/all_gather | solution.py:144
  577.4 26.0 %all-gather.32.cloned.1.call-done = bf16[352,2048]{1,0:T(8,128)(2,1)} async-done(((bf16[352,512]{1,0:T(8,128)(2,1)}), bf16[352,2048]{1,0:T(8,128)(2,1)}) %all-gather.32.cloned.1.call-update) | async-done | bytes 1441808 | tf_op jit(solution)/shard_map/all_gather | solution.py:145
  603.4 48.4 %all-gather.42.cloned.1.call-done = bf16[1,1024,2048]{2,1,0:T(8,128)(2,1)} async-done(((bf16[1,128,2048]{2,1,0:T(8,128)(2,1)}), bf16[1,1024,2048]{2,1,0:T(8,128)(2,1)}) %all-gather.42.cloned.1.call-update) | async-done | bytes 4194320 | tf_op jit(solution)/shard_map/all_gather | solution.py:223
  683.1 21.0 %copy.132 = bf16[1,864,2048]{2,0,1:T(2,128)(2,1)} copy(bf16[1,864,2048]{2,1,0:T(8,128)(2,1)S(1)} %fusion.55) | data formatting | bytes 7077888 | tf_op jit(solution)/shard_map/convert_element_type | solution.py:329
  704.6 76.9 %reduce.2 = bf16[864,2048]{1,0:T(8,128)(2,1)} reduce(bf16[864,1,2048]{2,1,0:T(2,128)(2,1)} %bitcast.225, bf16[]{:T(256)} %broadcast.305), dimensions={1}, to_apply=%bitcast.193.reduce_sub_computation | reduce | bytes 7077890
  788.7 84.4 %all_to_all.16 = bf16[8,2,110592]{2,1,0:T(2,128)(2,1)} all-to-all(bf16[8,2,110592]{2,1,0:T(2,128)(2,1)} %reshape.443), channel_id=1, replica_groups=mesh['shard'=4,'seq'=8] {'seq'}, dimensions={0} | all-to-all | bytes 7077888 | tf_op jit(solution)/shard_map/all_to_all | solution.py:80
  890.0 45.8 %all-gather.40.cloned.1.call-done = bf16[1024,2048]{1,0:T(8,128)(2,1)} async-done(((bf16[128,2048]{1,0:T(8,128)(2,1)}), bf16[1024,2048]{1,0:T(8,128)(2,1)}) %all-gather.40.cloned.1.call-update) | async-done | bytes 4194320 | tf_op jit(solution)/shard_map/all_gather | solution.py:335
  940.1 66.2 %while.28 = (s32[]{:T(128)}, f32[1024,2,192]{0,2,1:T(8,128)}, f32[1024,2,128]{0,2,1:T(8,128)}, f32[2,512,2,192]{1,0,3,2:T(2,128)}, s32[2]{0:T(128)S(1)}, /*index...) while((s32[]{:T(128)}, f32[1024,2,192]{0,2,1:T(8,128)}, ...), condition=%wide.region_15.16_spmd.clone, body=%wide.region_13.15_spmd.clone.sunk | while | flops 1762983424 | bytes 88113488 | solution.py:370
  958.1 15.0 dynamic_update_slice.20
  991.3 15.0 dynamic_update_slice.20
  1103.6 21.0 %copy.133 = bf16[1,864,2048]{2,0,1:T(2,128)(2,1)} copy(bf16[1,864,2048]{2,1,0:T(8,128)(2,1)S(1)} %convert_bitcast_fusion) | data formatting | bytes 7077888 | tf_op jit(solution)/shard_map/convert_element_type | solution.py:95
  1124.5 75.1 %reduce.1 = bf16[864,2048]{1,0:T(8,128)(2,1)S(1)} reduce(bf16[864,1,2048]{2,1,0:T(2,128)(2,1)} %bitcast.226, bf16[]{:T(256)} %broadcast.305), dimensions={1}, to_apply=%bitcast.194.reduce_sub_computation | reduce | bytes 7077890
  1215.9 81.0 %all-to-all-done.1 = bf16[8,2,110592]{2,1,0:T(2,128)(2,1)} async-done(((bf16[8,2,110592]{2,1,0:T(2,128)(2,1)}), bf16[8,2,110592]{2,1,0:T(2,128)(2,1)}, u32[]{:S(2)}, u32[]{:S(2)}) %all-to-all-start.1) | async-done | bytes 3538976 | tf_op jit(solution)/shard_map/all_to_all | solution.py:80
  1314.6 63.4 %reduce-scatter.45.cloned.1.call-done = bf16[1,512,1408]{2,1,0:T(8,128)(2,1)} async-done(((bf16[1,2048,1408]{2,1,0:T(8,128)(2,1)}), bf16[1,512,1408]{2,1,0:T(8,128)(2,1)}) %reduce-scatter.45.cloned.1.call-update) | async-done | bytes 1441808 | tf_op jit(solution)/shard_map/reduce_scatter | solution.py:431
  1381.2 65.5 %reduce-scatter.47.cloned.1.call-done = bf16[1,1408,512]{2,1,0:T(8,128)(2,1)} async-done(((bf16[1,1408,2048]{2,1,0:T(8,128)(2,1)}), bf16[1,1408,512]{2,1,0:T(8,128)(2,1)}) %reduce-scatter.47.cloned.1.call-update) | async-done | bytes 1441808 | tf_op jit(solution)/shard_map/reduce_scatter | solution.py:434
  1450.1 25.0 %reduce-scatter.33.cloned.1.call-done = bf16[128,512]{1,0:T(8,128)(2,1)} async-done(((bf16[512,512]{1,0:T(8,128)(2,1)}), bf16[128,512]{1,0:T(8,128)(2,1)}) %reduce-scatter.33.cloned.1.call-update) | async-done | bytes 131088 | tf_op jit(solution)/shard_map/reduce_scatter | solution.py:413
  1476.8 29.1 %reduce-scatter.35.cloned.1.call-done = bf16[256,512]{1,0:T(8,128)(2,1)} async-done(((bf16[256,2048]{1,0:T(8,128)(2,1)}), bf16[256,512]{1,0:T(8,128)(2,1)}) %reduce-scatter.35.cloned.1.call-update) | async-done | bytes 262160 | tf_op jit(solution)/shard_map/reduce_scatter | solution.py:416
  1507.6 32.3 %reduce-scatter.29.cloned.1.call-done = bf16[512,384]{1,0:T(8,128)(2,1)} async-done(((bf16[2048,384]{1,0:T(8,128)(2,1)}), bf16[512,384]{1,0:T(8,128)(2,1)}) %reduce-scatter.29.cloned.1.call-update) | async-done | bytes 393232 | tf_op jit(solution)/shard_map/reduce_scatter | solution.py:410
  1541.9 50.3 %reduce-scatter.27.cloned.1.call-done = bf16[128,2048]{1,0:T(8,128)(2,1)} async-done(((bf16[1024,2048]{1,0:T(8,128)(2,1)}), bf16[128,2048]{1,0:T(8,128)(2,1)}) %reduce-scatter.27.cloned.1.call-update) | async-done | bytes 524304 | tf_op jit(solution)/shard_map/reduce_scatter | solution.py:390
  1596.1 38.4 %all-reduce.6 = (f32[2048]{0:T(1024)S(1)}, f32[512]{0:T(512)S(1)}, f32[2048]{0:T(1024)S(1)}) all-reduce(f32[2048]{0:T(1024)S(1)} %get-tuple-element.197, f32[512]{0:T(512)S(1)} %copy-done.49, f32[2048]{0:T(1024)S(1)} %copy-done.50), channel_id=9, replica_groups=mesh['shard'=4,'seq'=8] {'shard','seq'}, use_global_device_ids=true, to_apply=%region_23.24.clone | all-reduce | flops 4608 | bytes 36864
  1639.3 100.8 %reduce-scatter.31.cloned.1.call-done = f32[64,576]{1,0:T(8,128)} async-done(((f32[2048,576]{1,0:T(8,128)}), f32[64,576]{1,0:T(8,128)}) %reduce-scatter.31.cloned.1.call-update) | async-done | bytes 147472 | tf_op jit(solution)/shard_map/reduce_scatter | solution.py:451
  (393 shorter events, 385.9 us)
Async XLA Ops:
  7.2 64.2 %all-gather.20.cloned.1.call-start = ((), (), s32[]{:S(2)}) async-start(), calls=%async_computation.22 | async-start | bytes 2703360 | tf_op jit(solution)/shard_map/all_gather | solution.py:132
  7.9 94.7 %all-gather.22.cloned.1.call-start = ((), (), s32[]{:S(2)}) async-start(), calls=%async_computation.23 | async-start | bytes 1179648 | tf_op jit(solution)/shard_map/all_gather | solution.py:173
  76.5 102.6 %all-gather.16.cloned.1.call-start = ((), (), s32[]{:S(2)}) async-start(), calls=%async_computation.20 | async-start | bytes 4718592 | tf_op jit(solution)/shard_map/all_gather | solution.py:172
  77.0 128.9 %all-gather.24.cloned.1.call-start = ((), (), s32[]{:S(2)}) async-start(), calls=%async_computation.24 | async-start | bytes 1310720 | tf_op jit(solution)/shard_map/all_gather | solution.py:142
  77.6 182.9 %reduce-scatter.21.cloned.1.call-start = ((), (), s32[]{:S(2)}) async-start(), calls=%async_computation.25 | async-start | bytes 4718592 | tf_op jit(solution)/shard_map/reduce_scatter | solution.py:212
  210.4 159.7 %all-gather.38.cloned.1.call-start = ((), (), s32[]{:S(2)}) async-start(), calls=%async_computation.33 | async-start | bytes 7208960 | tf_op jit(solution)/shard_map/all_gather | solution.py:148
  211.2 240.3 %all-gather.36.cloned.1.call-start = ((), (), s32[]{:S(2)}) async-start(), calls=%async_computation.32 | async-start | bytes 7208960 | tf_op jit(solution)/shard_map/all_gather | solution.py:147
  211.9 249.9 %all-gather.34.cloned.1.call-start = ((), (), s32[]{:S(2)}) async-start(), calls=%async_computation.31 | async-start | bytes 7208960 | tf_op jit(solution)/shard_map/all_gather | solution.py:146
  212.7 280.1 %all-gather.28.cloned.1.call-start = ((), (), s32[]{:S(2)}) async-start(), calls=%async_computation.27 | async-start | bytes 1802240 | tf_op jit(solution)/shard_map/all_gather | solution.py:143
  213.3 328.5 %all-gather.26.cloned.1.call-start = ((), (), s32[]{:S(2)}) async-start(), calls=%async_computation.26 | async-start | bytes 4718592 | tf_op jit(solution)/shard_map/all_gather | solution.py:222
  272.0 87.4 %all-to-all-start.2 = ((bf16[8,108,2048]{2,1,0:T(8,128)(2,1)}), bf16[8,108,2048]{2,1,0:T(8,128)(2,1)}, u32[]{:S(2)}, u32[]{:S(2)}) async-start(bf16[8,108,2048]{2,1,0:T(8,128)(2,1)} %reshape.421), calls=%async_computation.5 | async-start | bytes 7340032 | tf_op jit(solution)/shard_map/all_to_all | solution.py:76
  276.7 295.3 %all-gather.30.cloned.1.call-start = ((), (), s32[]{:S(2)}) async-start(), calls=%async_computation.28 | async-start | bytes 1802240 | tf_op jit(solution)/shard_map/all_gather | solution.py:144
  359.4 87.4 %all-to-all-start = ((bf16[8,108,2048]{2,1,0:T(8,128)(2,1)}), bf16[8,108,2048]{2,1,0:T(8,128)(2,1)}, u32[]{:S(2)}, u32[]{:S(2)}) async-start(bf16[8,108,2048]{2,1,0:T(8,128)(2,1)} %reshape.413), calls=%async_computation.2 | async-start | bytes 7340032 | tf_op jit(solution)/shard_map/all_to_all | solution.py:76
  364.1 239.3 %all-gather.32.cloned.1.call-start = ((), (), s32[]{:S(2)}) async-start(), calls=%async_computation.29 | async-start | bytes 1802240 | tf_op jit(solution)/shard_map/all_gather | solution.py:145
  364.8 286.9 %all-gather.42.cloned.1.call-start = ((), (), s32[]{:S(2)}) async-start(), calls=%async_computation.47 | async-start | bytes 4718592 | tf_op jit(solution)/shard_map/all_gather | solution.py:223
  365.4 515.9 %reduce-scatter.25.cloned.1.call-start = ((), (), s32[]{:S(2)}) async-start(), calls=%async_computation.34 | async-start | bytes 4718592 | tf_op jit(solution)/shard_map/reduce_scatter | solution.py:285
  665.2 270.5 %all-gather.40.cloned.1.call-start = ((), (), s32[]{:S(2)}) async-start(), calls=%async_computation.35 | async-start | bytes 4718592 | tf_op jit(solution)/shard_map/all_gather | solution.py:335
  889.9 196.2 %reduce-scatter.51.cloned.1.call-start = ((), (), s32[]{:S(2)}) async-start(), calls=%async_computation.49 | async-start | bytes 294912
  1008.9 78.3 %reduce-scatter.49.cloned.1.call-start = ((), (), s32[]{:S(2)}) async-start(), calls=%async_computation.48 | async-start | bytes 1179648
  1011.9 198.2 %reduce-scatter.37.cloned.1.call-start = ((), (), s32[]{:S(2)}) async-start(), calls=%async_computation.41 | async-start | bytes 1802240 | tf_op jit(solution)/shard_map/reduce_scatter | solution.py:419
  1017.0 195.0 %reduce-scatter.39.cloned.1.call-start = ((), (), s32[]{:S(2)}) async-start(), calls=%async_computation.42 | async-start | bytes 1802240 | tf_op jit(solution)/shard_map/reduce_scatter | solution.py:422
  1022.2 191.8 %reduce-scatter.41.cloned.1.call-start = ((), (), s32[]{:S(2)}) async-start(), calls=%async_computation.43 | async-start | bytes 1802240 | tf_op jit(solution)/shard_map/reduce_scatter | solution.py:425
  1027.5 277.6 %reduce-scatter.23.cloned.1.call-start = ((), (), s32[]{:S(2)}) async-start(), calls=%async_computation.30 | async-start | bytes 4718592 | tf_op jit(solution)/shard_map/reduce_scatter | solution.py:228
  1032.0 279.6 %reduce-scatter.43.cloned.1.call-start = ((), (), s32[]{:S(2)}) async-start(), calls=%async_computation.44 | async-start | bytes 7208960 | tf_op jit(solution)/shard_map/reduce_scatter | solution.py:428
  1044.1 333.9 %reduce-scatter.45.cloned.1.call-start = ((), (), s32[]{:S(2)}) async-start(), calls=%async_computation.45 | async-start | bytes 7208960 | tf_op jit(solution)/shard_map/reduce_scatter | solution.py:431
  1054.4 392.3 %reduce-scatter.47.cloned.1.call-start = ((), (), s32[]{:S(2)}) async-start(), calls=%async_computation.46 | async-start | bytes 7208960 | tf_op jit(solution)/shard_map/reduce_scatter | solution.py:434
  1066.1 409.0 %reduce-scatter.33.cloned.1.call-start = ((), (), s32[]{:S(2)}) async-start(), calls=%async_computation.39 | async-start | bytes 655360 | tf_op jit(solution)/shard_map/reduce_scatter | solution.py:413
  1069.2 436.7 %reduce-scatter.35.cloned.1.call-start = ((), (), s32[]{:S(2)}) async-start(), calls=%async_computation.40 | async-start | bytes 1310720 | tf_op jit(solution)/shard_map/reduce_scatter | solution.py:416
  1073.8 466.1 %reduce-scatter.29.cloned.1.call-start = ((), (), s32[]{:S(2)}) async-start(), calls=%async_computation.37 | async-start | bytes 1966080 | tf_op jit(solution)/shard_map/reduce_scatter | solution.py:410
  1081.4 510.9 %reduce-scatter.27.cloned.1.call-start = ((), (), s32[]{:S(2)}) async-start(), calls=%async_computation.36 | async-start | bytes 4718592 | tf_op jit(solution)/shard_map/reduce_scatter | solution.py:390
  1085.8 654.3 %reduce-scatter.31.cloned.1.call-start = ((), (), s32[]{:S(2)}) async-start(), calls=%async_computation.38 | async-start | bytes 5406720 | tf_op jit(solution)/shard_map/reduce_scatter | solution.py:451
  1205.3 91.5 %all-to-all-start.1 = ((bf16[8,2,110592]{2,1,0:T(2,128)(2,1)}), bf16[8,2,110592]{2,1,0:T(2,128)(2,1)}, u32[]{:S(2)}, u32[]{:S(2)}) async-start(bf16[8,2,110592]{2,1,0:T(2,128)(2,1)} %reshape.441), calls=%async_computation.3 | async-start | bytes 7077888 | tf_op jit(solution)/shard_map/all_to_all | solution.py:80
  (81 other events, 5177.7 us)
Sparse Core Ops, SparseCore 0:
  10.8 60.5 all-gather.19
  75.8 23.0 all-gather.21
  100.8 29.2 all-gather.17
  132.1 46.8 all-gather.15
  180.7 25.1 all-gather.23
  210.5 49.9 reduce-scatter.20
  262.3 63.9 all-gather.37
  328.2 65.6 all-gather.35
  395.7 65.6 all-gather.33
  463.1 29.6 all-gather.27
  494.9 46.8 all-gather.25
  543.5 28.4 all-gather.29
  573.8 29.6 all-gather.31
  604.9 46.8 all-gather.41
  665.3 48.7 reduce-scatter.24
  890.0 45.7 all-gather.39
  1009.0 29.6 reduce-scatter.50
  1041.4 30.7 reduce-scatter.48
  1075.1 28.4 reduce-scatter.36
  1106.4 30.2 reduce-scatter.38
  1139.7 30.2 reduce-scatter.40
  1172.3 55.7 reduce-scatter.22
  1231.1 78.3 reduce-scatter.42
  1312.3 65.6 reduce-scatter.44
  1381.0 65.6 reduce-scatter.46
  1450.0 25.0 reduce-scatter.32
  1477.8 27.9 reduce-scatter.34
  1508.8 31.1 reduce-scatter.28
  1542.3 49.8 reduce-scatter.26
  1594.9 145.1 reduce-scatter.30
where the time goes:
time: 1760 us; the launch traced here: 1750 us
  waiting for transfers between devices  941 us (53%)
  matrix products  232 us (13%)
  other arithmetic  200 us (11%)
  blocking collectives  189 us (11%)
  local copies, waits for them, and re-layouts  145 us (8%)
    unnamed x4, other arithmetic  152 us
    all_to_all x2, waiting for transfers between devices, to_experts(): lax.all_to_all(buffer, 'seq', split_axis=0, concat_axis=1, tiled=True)  140 us
    reduce_scatter x1, waiting for transfers between devices, on_device(): lax.psum_scatter(d_wlatent, ('shard', 'seq'), scatter_dimension=0, tiled=...  101 us
    all_to_all x1, blocking collectives, to_sources(): lax.all_to_all(buffer, 'seq', split_axis=1, concat_axis=0, tiled=True)  84.4 us
    all_to_all x1, waiting for transfers between devices, to_sources(): lax.all_to_all(buffer, 'seq', split_axis=1, concat_axis=0, tiled=True)  81 us
    unnamed x2, blocking collectives  80.7 us
    reduce_scatter x1, waiting for transfers between devices, on_device(): lax.psum_scatter(d_edown.astype(jnp.bfloat16), 'shard', scatter_dimension...  65.5 us
    reduce_scatter x1, waiting for transfers between devices, on_device(): lax.psum_scatter(expert_up_output_grad.astype(jnp.bfloat16), 'shard', sca...  63.4 us
  transfers between devices with their start and end apart: 33, of which 21 were waited for; matrix products, arithmetic and copies ran while one was open for 27% of the time, Pallas kernels for 0%

commit v1 on v0

v1 whole, which is shorter than its diff:
```python
import jax
import jax.numpy as jnp
from jax import lax
from jax.sharding import PartitionSpec as P

HEADS = 16
NOPE = 128
ROPE = 64
VDIM = 128
RANK = 512
TOPK = 6
EXP_DEV = 1


EPSILON = 1e-06
THETA = 10000.0
MASKED = -1e30


def rope_tables(positions, depth):
    half_depth = depth // 2
    frequency = THETA ** (-(2.0 * jnp.arange(half_depth, dtype=jnp.float32)) / depth)
    angles = positions.astype(jnp.float32)[:, None] * frequency[None, :]
    return (jnp.cos(angles), jnp.sin(angles))


def rotate(values, cosine, sine):
    half_depth = values.shape[-1] // 2
    first = values[..., :half_depth]
    second = values[..., half_depth:]
    return jnp.concatenate([first * cosine - second * sine, second * cosine + first * sine], -1)


def norm_forward(values, scaling):
    inverse = lax.rsqrt(jnp.mean(values * values, -1, keepdims=True) + EPSILON)
    return (values * inverse * scaling, inverse)


def norm_backward(values, inverse, scaling, upstream):
    weighted = upstream * scaling
    scaling_grad = jnp.sum(upstream * values * inverse, 0)
    centre = jnp.mean(weighted * values, -1, keepdims=True)
    return (inverse * weighted - values * inverse**3 * centre, scaling_grad)


def swish_gradient(gate_pre, upper, upstream):
    sigma = jax.nn.sigmoid(gate_pre)
    return (
        upstream * upper * sigma * (1.0 + gate_pre * (1.0 - sigma)),
        upstream * gate_pre * sigma,
    )


def inner_rows(left, right):
    return lax.dot_general(
        left, right, (((0,), (0,)), ((), ())), preferred_element_type=jnp.float32
    )


def times_transposed(left, right):
    return lax.dot_general(
        left, right, (((1,), (1,)), ((), ())), preferred_element_type=jnp.float32
    )


def masked_scores(queries, keys, offset, score_scale):
    scores = (
        jnp.einsum("qhd,khd->hqk", queries, keys, preferred_element_type=jnp.float32) * score_scale
    )
    query_pos = offset + jnp.arange(queries.shape[0])
    seen = jnp.arange(keys.shape[0])[None, :] <= query_pos[:, None]
    return jnp.where(seen[None], scores, MASKED)


def gather_seq(block):
    return lax.all_gather(block, "seq", axis=0, tiled=True)


def scatter_seq(partial):
    return lax.psum_scatter(partial, "seq", scatter_dimension=0, tiled=True)


def rows_dot(left, right):
    return jnp.dot(left, right, preferred_element_type=jnp.float32)


def on_device(
    inputs,
    attn_gain,
    query_project_weight,
    latent_project_weight,
    latent_gain,
    latent_keyval_weight,
    attention_output_weight,
    ffn_gain,
    shared_gate,
    shared_up,
    shared_down,
    expert_gate,
    expert_up,
    expert_down,
    routes,
    slots,
    gates,
    cotangent,
):
    tok_rows = inputs.shape[1]
    model_width = inputs.shape[2]
    groups = lax.axis_size("seq")
    shards = lax.axis_size("shard")
    me = lax.axis_index("seq")
    local_heads = HEADS // groups
    query_width = NOPE + ROPE
    experts = EXP_DEV * groups
    capacity = 9 * tok_rows * TOPK // (8 * experts)
    length = tok_rows * groups
    score_scale = (NOPE + ROPE) ** (-0.5)
    block_rows = min(512, length)
    starts = jnp.arange(length // block_rows) * block_rows
    own_start = me * tok_rows

    def gather_shard(weight, axis):
        return lax.all_gather(weight, "shard", axis=axis, tiled=True)

    own_inputs = inputs.reshape(tok_rows, model_width)
    upstream = cotangent.reshape(tok_rows, model_width)
    route_rows = routes.reshape(tok_rows, TOPK)
    slot_rows = slots.reshape(tok_rows, TOPK)
    kept = (route_rows[:, :, None] == jnp.arange(experts)[None, None, :]) & (
        slot_rows < capacity
    )[:, :, None]
    gate_table = jnp.sum(
        jnp.where(kept, gates.reshape(tok_rows, TOPK).astype(jnp.float32)[:, :, None], 0.0), 1
    ).astype(jnp.bfloat16)

    gains = lax.all_gather(
        jnp.concatenate([attn_gain, latent_gain, ffn_gain]), ("shard", "seq"), axis=0, tiled=False
    ).astype(jnp.float32)
    one_width = attn_gain.shape[0]
    lat_width = latent_gain.shape[0]
    first_norm_weight = gains[:, :one_width].reshape(-1)
    latent_norm_weight = gains[:, one_width : one_width + lat_width].reshape(-1)
    second_norm_weight = gains[:, one_width + lat_width :].reshape(-1)
    full_latent = lax.all_gather(latent_project_weight, ("shard", "seq"), axis=0, tiled=True)

    inputs_all = gather_seq(own_inputs)
    full_query = gather_shard(query_project_weight, 0)
    full_kvup = gather_shard(latent_keyval_weight, 0)
    full_out = gather_shard(attention_output_weight, 1)
    upstream_all = gather_seq(upstream)
    table_all = gather_seq(gate_table)
    full_sgate = gather_shard(shared_gate, 0)
    full_sup = gather_shard(shared_up, 0)
    full_sdown = gather_shard(shared_down, 1)
    full_egate = gather_shard(expert_gate[0], 0)
    full_eup = gather_shard(expert_up[0], 0)
    full_edown = gather_shard(expert_down[0], 1)
    gate_column = lax.dynamic_slice_in_dim(table_all, me, 1, 1).astype(jnp.float32)

    residual_stream = own_inputs.astype(jnp.float32)
    first_all = norm_forward(inputs_all.astype(jnp.float32), first_norm_weight)[0].astype(
        jnp.bfloat16
    )
    cos_all, sin_all = rope_tables(jnp.arange(length), ROPE)
    latent = rows_dot(first_all, full_latent)
    latent_all = norm_forward(latent[:, :RANK], latent_norm_weight)[0].astype(jnp.bfloat16)
    rope_all = rotate(latent[:, RANK:], cos_all, sin_all).astype(jnp.bfloat16)
    head_query = rows_dot(first_all, full_query).reshape(length, local_heads, query_width)
    head_query = jnp.concatenate(
        [
            head_query[..., :NOPE],
            rotate(head_query[..., NOPE:], cos_all[:, None], sin_all[:, None]),
        ],
        -1,
    ).astype(jnp.bfloat16)
    keyval = (
        rows_dot(latent_all, full_kvup)
        .astype(jnp.bfloat16)
        .reshape(length, local_heads, NOPE + VDIM)
    )
    head_keys = jnp.concatenate(
        [keyval[..., :NOPE], jnp.broadcast_to(rope_all[:, None, :], (length, local_heads, ROPE))],
        -1,
    )
    head_values = keyval[..., NOPE:]

    def forward_block(offset):
        queries = lax.dynamic_slice_in_dim(head_query, offset, block_rows, 0)
        scores = masked_scores(queries, head_keys, offset, score_scale)
        top = jnp.max(scores, -1, keepdims=True)
        expo = jnp.exp(scores - top)
        total = jnp.sum(expo, -1, keepdims=True)
        probs_low = (expo / total).astype(jnp.bfloat16)
        result = jnp.einsum(
            "hqk,khd->qhd", probs_low, head_values, preferred_element_type=jnp.float32
        ).astype(jnp.bfloat16)
        return (result, (top + jnp.log(total))[..., 0])

    attended_blocks, log_totals = lax.map(forward_block, starts)
    attended = attended_blocks.reshape(length, local_heads * VDIM)
    middle = residual_stream + scatter_seq(
        rows_dot(attended, full_out).astype(jnp.bfloat16)
    ).astype(jnp.float32)
    normed_two, inv_two = norm_forward(middle, second_norm_weight)
    second_all = gather_seq(normed_two.astype(jnp.bfloat16))

    sgate_pre = rows_dot(second_all, full_sgate)
    sup_pre = rows_dot(second_all, full_sup)
    shidden = (jax.nn.silu(sgate_pre) * sup_pre).astype(jnp.bfloat16)
    d_sdown = inner_rows(shidden, upstream_all).astype(jnp.bfloat16)
    d_sgate, d_sup = swish_gradient(sgate_pre, sup_pre, times_transposed(upstream_all, full_sdown))
    d_sgate = d_sgate.astype(jnp.bfloat16)
    d_sup = d_sup.astype(jnp.bfloat16)
    d_wsgate = inner_rows(second_all, d_sgate).astype(jnp.bfloat16)
    d_wsup = inner_rows(second_all, d_sup).astype(jnp.bfloat16)

    egate_pre = rows_dot(second_all, full_egate)
    eup_pre = rows_dot(second_all, full_eup)
    ehidden = (jax.nn.silu(egate_pre) * eup_pre).astype(jnp.bfloat16)
    d_eoutput = (gate_column * upstream_all.astype(jnp.float32)).astype(jnp.bfloat16)
    d_edown = inner_rows(ehidden, d_eoutput).astype(jnp.bfloat16)
    d_egate, d_eup = swish_gradient(egate_pre, eup_pre, times_transposed(d_eoutput, full_edown))
    d_egate = d_egate.astype(jnp.bfloat16)
    d_eup = d_eup.astype(jnp.bfloat16)
    d_second = scatter_seq(
        (
            times_transposed(d_sgate, full_sgate)
            + times_transposed(d_sup, full_sup)
            + times_transposed(d_egate, full_egate)
            + times_transposed(d_eup, full_eup)
        ).astype(jnp.bfloat16)
    ).astype(jnp.float32)
    d_wegate = inner_rows(second_all, d_egate).astype(jnp.bfloat16)
    d_weup = inner_rows(second_all, d_eup).astype(jnp.bfloat16)
    eoutput = rows_dot(ehidden, full_edown).astype(jnp.bfloat16).astype(jnp.float32)
    added = scatter_seq(
        (rows_dot(shidden, full_sdown) + gate_column * eoutput).astype(jnp.bfloat16)
    ).astype(jnp.float32)
    output = (middle + added).astype(jnp.bfloat16).reshape(1, tok_rows, model_width)

    d_middle_norm, d_gain_two = norm_backward(middle, inv_two, second_norm_weight, d_second)
    d_middle = upstream.astype(jnp.float32) + d_middle_norm
    d_branch_all = gather_seq(d_middle.astype(jnp.bfloat16))
    d_wout = inner_rows(attended, d_branch_all).astype(jnp.bfloat16)
    d_heads = (
        times_transposed(d_branch_all, full_out)
        .astype(jnp.bfloat16)
        .reshape(length, local_heads, VDIM)
    )

    def backward_block(carry, element):
        offset, block_lse = element
        key_sum, value_sum = carry
        queries = lax.dynamic_slice_in_dim(head_query, offset, block_rows, 0)
        d_out = lax.dynamic_slice_in_dim(d_heads, offset, block_rows, 0)
        scores = masked_scores(queries, head_keys, offset, score_scale)
        probs = jnp.exp(scores - block_lse[..., None])
        probs_low = probs.astype(jnp.bfloat16)
        d_probs = jnp.einsum("qhd,khd->hqk", d_out, head_values, preferred_element_type=jnp.float32)
        centre = jnp.sum(probs * d_probs, -1, keepdims=True)
        d_scores = (probs * (d_probs - centre)).astype(jnp.bfloat16)
        d_queries = (
            jnp.einsum("hqk,khd->qhd", d_scores, head_keys, preferred_element_type=jnp.float32)
            * score_scale
        )
        key_sum = (
            key_sum
            + jnp.einsum("hqk,qhd->khd", d_scores, queries, preferred_element_type=jnp.float32)
            * score_scale
        )
        value_sum = value_sum + jnp.einsum(
            "hqk,qhd->khd", probs_low, d_out, preferred_element_type=jnp.float32
        )
        return ((key_sum, value_sum), d_queries)

    zero_keys = jnp.zeros((length, local_heads, query_width), jnp.float32)
    zero_values = jnp.zeros((length, local_heads, VDIM), jnp.float32)
    (d_keys, d_values), d_queries = lax.scan(
        backward_block, (zero_keys, zero_values), (starts, log_totals)
    )
    d_queries = d_queries.reshape(length, local_heads, query_width)
    d_queries = jnp.concatenate(
        [d_queries[..., :NOPE], rotate(d_queries[..., NOPE:], cos_all[:, None], -sin_all[:, None])],
        -1,
    )
    d_queries = d_queries.astype(jnp.bfloat16).reshape(length, local_heads * query_width)
    d_keys = d_keys.astype(jnp.bfloat16)
    d_values = d_values.astype(jnp.bfloat16)
    d_keyval = jnp.concatenate([d_keys[..., :NOPE], d_values], -1).reshape(
        length, local_heads * (NOPE + VDIM)
    )
    d_wkvup = inner_rows(latent_all, d_keyval).astype(jnp.bfloat16)
    d_wquery = inner_rows(first_all, d_queries).astype(jnp.bfloat16)
    first_part = times_transposed(d_queries, full_query).astype(jnp.bfloat16)
    latent_part = times_transposed(d_keyval, full_kvup).astype(jnp.bfloat16)
    rope_part = jnp.sum(d_keys[..., NOPE:].astype(jnp.float32), 1).astype(jnp.bfloat16)
    latent_back = scatter_seq(jnp.concatenate([latent_part, rope_part], -1)).astype(jnp.float32)
    first_back = scatter_seq(first_part).astype(jnp.float32)

    own_latent = lax.dynamic_slice_in_dim(latent, own_start, tok_rows, 0)[:, :RANK]
    cos_own = lax.dynamic_slice_in_dim(cos_all, own_start, tok_rows, 0)
    sin_own = lax.dynamic_slice_in_dim(sin_all, own_start, tok_rows, 0)
    inv_latent = norm_forward(own_latent, latent_norm_weight)[1]
    d_rope = rotate(latent_back[:, RANK:], cos_own, -sin_own)
    d_compressed, d_gain_latent = norm_backward(
        own_latent, inv_latent, latent_norm_weight, latent_back[:, :RANK]
    )
    d_latent = jnp.concatenate([d_compressed, d_rope], -1).astype(jnp.bfloat16)
    d_latent_all = gather_seq(d_latent)
    inv_one = norm_forward(residual_stream, first_norm_weight)[1]
    d_first = first_back + times_transposed(d_latent, full_latent)
    d_resid, d_gain_one = norm_backward(residual_stream, inv_one, first_norm_weight, d_first)
    input_grad = (d_middle + d_resid).reshape(1, tok_rows, model_width)
    own_columns = lax.dynamic_index_in_dim(
        first_all.reshape(length, shards, groups, one_width), me, 2, keepdims=False
    ).reshape(length, shards * one_width)
    d_wlatent = inner_rows(own_columns, d_latent_all).astype(jnp.bfloat16)

    def scatter_shard(grad, axis):
        return lax.psum_scatter(grad, "shard", scatter_dimension=axis, tiled=True).astype(
            jnp.float32
        )

    devices = shards * groups
    gain_grads = lax.psum_scatter(
        jnp.concatenate(
            [
                d_gain_one.reshape(devices, one_width),
                d_gain_latent.reshape(devices, lat_width),
                d_gain_two.reshape(devices, one_width),
            ],
            1,
        ),
        ("shard", "seq"),
        scatter_dimension=0,
        tiled=True,
    ).reshape(-1)
    return (
        output,
        input_grad,
        gain_grads[:one_width],
        scatter_shard(d_wquery, 0),
        scatter_shard(d_wlatent, 0),
        gain_grads[one_width : one_width + lat_width],
        scatter_shard(d_wkvup, 0),
        scatter_shard(d_wout, 1),
        gain_grads[one_width + lat_width :],
        scatter_shard(d_wsgate, 0),
        scatter_shard(d_wsup, 0),
        scatter_shard(d_sdown, 1),
        scatter_shard(d_wegate, 0)[None],
        scatter_shard(d_weup, 0)[None],
        scatter_shard(d_edown, 1)[None],
    )


def solution(mesh):
    in_specs = (
        P("shard", "seq", None),
        P(("shard", "seq")),
        P("shard", "seq"),
        P(("shard", "seq"), None),
        P(("shard", "seq")),
        P("shard", "seq"),
        P("seq", "shard"),
        P(("shard", "seq")),
        P("shard", "seq"),
        P("shard", "seq"),
        P("seq", "shard"),
        P("seq", "shard", None),
        P("seq", "shard", None),
        P("seq", None, "shard"),
        P("shard", "seq", None),
        P("shard", "seq", None),
        P("shard", "seq", None),
        P("shard", "seq", None),
    )
    out_specs = (
        P("shard", "seq", None),
        P("shard", "seq", None),
        P(("shard", "seq")),
        P("shard", "seq"),
        P(("shard", "seq"), None),
        P(("shard", "seq")),
        P("shard", "seq"),
        P("seq", "shard"),
        P(("shard", "seq")),
        P("shard", "seq"),
        P("shard", "seq"),
        P("seq", "shard"),
        P("seq", "shard", None),
        P("seq", "shard", None),
        P("seq", None, "shard"),
    )
    return jax.shard_map(
        on_device, mesh=mesh, in_specs=in_specs, out_specs=out_specs, check_vma=False
    )
```

time: 1760 us -> 1430 us (0.81)
  other arithmetic: 200 us -> 59.7 us
  local copies, waits for them, and re-layouts: 145 us -> 51.5 us
  blocking collectives: 189 us -> 111 us
    all_to_all x3 -> x0, waiting for transfers between devices: 221 us -> none  [the longest x2 140 us: to_experts(): lax.all_to_all(buffer, 'seq', split_axis=0, concat_axis=1, tiled=True)]
    unnamed x4 -> x2, other arithmetic: 152 us -> 0.01 us
    all_to_all x1 -> x0, blocking collectives: 84.4 us -> none  [to_sources(): lax.all_to_all(buffer, 'seq', split_axis=1, concat_axis=0, tiled=True)]
    reduce_scatter x14, waiting for transfers between devices: 414 us -> 495 us  [the longest x10 339 us: scatter_shard(): lax.psum_scatter(grad, 'shard', scatter_dimension=axis, tiled=True)]
    all_gather x13, waiting for transfers between devices: 284 us -> 359 us  [the longest x8 237 us: gather_shard(): return lax.all_gather(weight, 'shard', axis=axis, tiled=True)]
    dot_general x18 -> x10, matrix products: 134 us -> 68.8 us  [rows_dot(): return jnp.dot(left, right, preferred_element_type=jnp.float32)]
    convert_element_type x2 -> x1, local copies, waits for them, and re-layouts: 41.9 us -> 0.09 us  [on_device(): gains = lax.all_gather(jnp.concatenate([attn_gain, latent_gain, ffn_gain]...]
    all_gather x1, waiting for transfers between devices: 15.4 us -> 55 us  [on_device(): lax.all_gather(latent_project_weight, ('shard', 'seq'), axis=0, tiled=True)]
  transfers between devices with their start and end apart: 33 -> 29, of which waited for: 21 -> 24; matrix products, arithmetic and copies ran while one was open for 27% -> 16% of each run, Pallas kernels for 0% -> 0%
where the time goes in v1:
time: 1430 us
  waiting for transfers between devices  947 us (66%)
  matrix products  232 us (16%)
  blocking collectives  111 us (8%)
  other arithmetic  59.7 us (4%)
  local copies, waits for them, and re-layouts  51.5 us (4%)
  between operations  15.2 us (1%)
    reduce_scatter x10, waiting for transfers between devices, scatter_shard(): lax.psum_scatter(grad, 'shard', scatter_dimension=axis, tiled=True)  339 us
    all_gather x8, waiting for transfers between devices, gather_shard(): return lax.all_gather(weight, 'shard', axis=axis, tiled=True)  237 us
    reduce_scatter x4, waiting for transfers between devices, scatter_seq(): return lax.psum_scatter(partial, 'seq', scatter_dimension=0, tiled=True)  155 us
    all_gather x5, waiting for transfers between devices, gather_seq(): return lax.all_gather(block, 'seq', axis=0, tiled=True)  122 us
    unnamed x2, blocking collectives  86 us
    dot_general x10, matrix products, rows_dot(): return jnp.dot(left, right, preferred_element_type=jnp.float32)  68.8 us
    dot_general x10, matrix products, times_transposed(): lax.dot_general(left, right, (((1,), (1,)), ((), ())), preferred_element_...  64.4 us
    dot_general x10, matrix products, inner_rows(): lax.dot_general(left, right, (((0,), (0,)), ((), ())), preferred_element_...  64 us
  transfers between devices with their start and end apart: 29, of which 24 were waited for; matrix products, arithmetic and copies ran while one was open for 16% of the time, Pallas kernels for 0%

profile of v1, /device:TPU:0, one launch (start us, length us, event | category | flops | bytes accessed | tf_op | source)
XLA Modules:
  0.0 1426.7 jit_solution(4804565590978271707)
XLA Ops:
  12.5 46.4 %all-reduce = bf16[4608]{0:T(1024)(128)(2,1)S(1)} all-reduce(bf16[4608]{0:T(1024)(128)(2,1)S(1)} %dynamic-update-slice), channel_id=3, replica_groups=mesh['shard'=4,'seq'=8] {'shard','seq'}, use_global_device_ids=true, to_apply=%add | all-reduce | flops 4608 | bytes 18432
  77.0 15.7 %all-gather.21.cloned.1.call-done = bf16[2048,384]{1,0:T(8,128)(2,1)} async-done(((bf16[512,384]{1,0:T(8,128)(2,1)}), bf16[2048,384]{1,0:T(8,128)(2,1)}) %all-gather.21.cloned.1.call-update) | async-done | bytes 1572880 | tf_op jit(solution)/shard_map/all_gather | solution.py:123
  98.4 55.0 %all-gather.23.cloned.1.call-done = bf16[2048,576]{1,0:T(8,128)(2,1)} async-done(((bf16[64,576]{1,0:T(8,128)(2,1)}), bf16[2048,576]{1,0:T(8,128)(2,1)}) %all-gather.23.cloned.1.call-update) | async-done | bytes 2359312 | tf_op jit(solution)/shard_map/all_gather | solution.py:144
  166.2 20.3 %while.27 = (s32[]{:T(128)}, bf16[2,512,2,128]{3,2,1,0:T(2,128)(2,1)S(1)}, f32[2,2,512]{2,1,0:T(2,128)S(1)}, s32[2]{0:T(128)S(1)}, bf16[1024,2,192]{0,2,1:T(8,12...) while((s32[]{:T(128)}, ...), condition=%wide.region_5.6_spmd, body=%wide.region_2.5_spmd.sunk | while | flops 684326400 | bytes 17207468 | solution.py:199
  193.6 46.7 %reduce-scatter.18.cloned.1.call-done = bf16[128,2048]{1,0:T(8,128)(2,1)} async-done(((bf16[1024,2048]{1,0:T(8,128)(2,1)}), bf16[128,2048]{1,0:T(8,128)(2,1)}) %reduce-scatter.18.cloned.1.call-update) | async-done | bytes 524304 | tf_op jit(solution)/shard_map/reduce_scatter | solution.py:80
  246.4 13.5 all_gather.65
  259.9 27.3 %all-gather.47.cloned.1.call-done = bf16[1,1024,2048]{2,1,0:T(8,128)(2,1)} async-done(((bf16[1,128,2048]{2,1,0:T(8,128)(2,1)}), bf16[1,1024,2048]{2,1,0:T(8,128)(2,1)}) %all-gather.47.cloned.1.call-update) | async-done | bytes 4194320 | tf_op jit(solution)/shard_map/all_gather | solution.py:76
  287.2 66.2 %all-gather.45.cloned.1.call-done = bf16[1,1408,2048]{2,1,0:T(8,128)(2,1)} async-done(((bf16[1,1408,512]{2,1,0:T(8,128)(2,1)}), bf16[1,1408,2048]{2,1,0:T(8,128)(2,1)}) %all-gather.45.cloned.1.call-update) | async-done | bytes 5767184 | tf_op jit(solution)/shard_map/all_gather | solution.py:123
  353.4 11.9 fusion.39
  365.3 55.6 %all-gather.43.cloned.1.call-done = bf16[1,2048,1408]{2,1,0:T(8,128)(2,1)} async-done(((bf16[1,512,1408]{2,1,0:T(8,128)(2,1)}), bf16[1,2048,1408]{2,1,0:T(8,128)(2,1)}) %all-gather.43.cloned.1.call-update) | async-done | bytes 5767184 | tf_op jit(solution)/shard_map/all_gather | solution.py:123
  420.9 49.1 %all-gather.27.cloned.1.call-done = bf16[1024,2048]{1,0:T(8,128)(2,1)} async-done(((bf16[128,2048]{1,0:T(8,128)(2,1)}), bf16[1024,2048]{1,0:T(8,128)(2,1)}) %all-gather.27.cloned.1.call-update) | async-done | bytes 4194320 | tf_op jit(solution)/shard_map/all_gather | solution.py:76
  470.0 11.7 fusion.45
  481.7 54.5 %all-gather.41.cloned.1.call-done = bf16[1,2048,1408]{2,1,0:T(8,128)(2,1)} async-done(((bf16[1,512,1408]{2,1,0:T(8,128)(2,1)}), bf16[1,2048,1408]{2,1,0:T(8,128)(2,1)}) %all-gather.41.cloned.1.call-update) | async-done | bytes 5767184 | tf_op jit(solution)/shard_map/all_gather | solution.py:123
  536.2 16.5 %multiply_convert_fusion.3 = (bf16[1024,1408]{1,0:T(8,128)(2,1)}, bf16[1024,1408]{1,0:T(8,128)(2,1)}, bf16[1024,1408]{1,0:T(8,128)(2,1)S(1)}) fusion(f32[1024,1408]{1,0:T(8,128)} %fusion.39, f32[1024,1408]{1,0:T(8,128)} %fusion.45, bf16[1024,2048]{1,0:T(8,128)(2,1)} %all-gather.27.cloned.1.call-done, bf16[1,2048,1408]{2,1,0:T(8,128)(2,1)} %all-gather.41.cloned.1.call-done), kind=kOutput, calls=%fused_computation.70 | convolution fusion | flops 5928648704 | bytes 30146560 | tf_op jit(solution)/shard_map/dot_general | solution.py:84
  573.1 25.9 %all-gather.31.cloned.1.call-done = bf16[2048,352]{0,1:T(8,128)(2,1)} async-done(((bf16[512,352]{0,1:T(8,128)(2,1)}), bf16[2048,352]{0,1:T(8,128)(2,1)}) %all-gather.31.cloned.1.call-update) | async-done | bytes 1441808 | tf_op jit(solution)/shard_map/all_gather | solution.py:123
  615.2 15.3 %all-gather.33.cloned.1.call-done = bf16[352,2048]{1,0:T(8,128)(2,1)} async-done(((bf16[352,512]{1,0:T(8,128)(2,1)}), bf16[352,2048]{1,0:T(8,128)(2,1)}) %all-gather.33.cloned.1.call-update) | async-done | bytes 1441808 | tf_op jit(solution)/shard_map/all_gather | solution.py:123
  651.1 49.9 %reduce-scatter.22.cloned.1.call-done = bf16[128,2048]{1,0:T(8,128)(2,1)} async-done(((bf16[1024,2048]{1,0:T(8,128)(2,1)}), bf16[128,2048]{1,0:T(8,128)(2,1)}) %reduce-scatter.22.cloned.1.call-update) | async-done | bytes 524304 | tf_op jit(solution)/shard_map/reduce_scatter | solution.py:80
  705.4 45.4 %all-gather.35.cloned.1.call-done = bf16[1024,2048]{1,0:T(8,128)(2,1)} async-done(((bf16[128,2048]{1,0:T(8,128)(2,1)}), bf16[1024,2048]{1,0:T(8,128)(2,1)}) %all-gather.35.cloned.1.call-update) | async-done | bytes 4194320 | tf_op jit(solution)/shard_map/all_gather | solution.py:76
  755.1 66.2 %while.28 = (s32[]{:T(128)}, f32[1024,2,192]{0,2,1:T(8,128)}, f32[1024,2,128]{0,2,1:T(8,128)}, f32[2,512,2,192]{1,0,3,2:T(2,128)}, s32[2]{0:T(128)S(1)}, /*index...) while((s32[]{:T(128)}, f32[1024,2,192]{0,2,1:T(8,128)}, ...), condition=%wide.region_15.16_spmd.clone, body=%wide.region_13.15_spmd.clone.sunk | while | flops 1762983424 | bytes 88113488 | solution.py:278
  773.0 14.9 %dynamic_update_slice.20 = f32[2,512,2,192]{1,0,3,2:T(2,128)} dynamic-update-slice(f32[2,512,2,192]{1,0,3,2:T(2,128)} %get-tuple-element.424, f32[1,512,2,192]{1,0,3,2:T(1,128)S(1)} %copy.104, s32[]{:T(128)S(6)} %copy.122, s32[]{:T(128)} %constant.34.clone.1..sunk.1, s32[]{:T(128)} %constant.34.clone.1..sunk.1, s32[]{:T(128)} %constant.34.clone.1..sunk.1) | dynamic-update-slice | bytes 1572868 | tf_op jit(solution)/shard_map/while/body/jit(dynamic_update_index_in_dim)/dynamic_update_slice | solution.py:278
  806.3 14.9 %dynamic_update_slice.20 = f32[2,512,2,192]{1,0,3,2:T(2,128)} dynamic-update-slice(f32[2,512,2,192]{1,0,3,2:T(2,128)} %get-tuple-element.424, f32[1,512,2,192]{1,0,3,2:T(1,128)S(1)} %copy.104, s32[]{:T(128)S(6)} %copy.122, s32[]{:T(128)} %constant.34.clone.1..sunk.1, s32[]{:T(128)} %constant.34.clone.1..sunk.1, s32[]{:T(128)} %constant.34.clone.1..sunk.1) | dynamic-update-slice | bytes 1572868 | tf_op jit(solution)/shard_map/while/body/jit(dynamic_update_index_in_dim)/dynamic_update_slice | solution.py:278
  826.6 32.3 %reduce-scatter.46.cloned.1.call-done = bf16[128,576]{1,0:T(8,128)(2,1)} async-done(((bf16[1024,576]{1,0:T(8,128)(2,1)}), bf16[128,576]{1,0:T(8,128)(2,1)}) %reduce-scatter.46.cloned.1.call-update) | async-done | bytes 147472
  956.3 28.9 %reduce-scatter.38.cloned.1.call-done = bf16[352,512]{1,0:T(8,128)(2,1)} async-done(((bf16[352,2048]{1,0:T(8,128)(2,1)}), bf16[352,512]{1,0:T(8,128)(2,1)}) %reduce-scatter.38.cloned.1.call-update) | async-done | bytes 360464 | tf_op jit(solution)/shard_map/reduce_scatter | solution.py:320
  987.2 66.7 %reduce-scatter.40.cloned.1.call-done = bf16[512,1408]{1,0:T(8,128)(2,1)} async-done(((bf16[2048,1408]{1,0:T(8,128)(2,1)}), bf16[512,1408]{1,0:T(8,128)(2,1)}) %reduce-scatter.40.cloned.1.call-update) | async-done | bytes 1441808 | tf_op jit(solution)/shard_map/reduce_scatter | solution.py:320
  1057.1 65.6 %reduce-scatter.42.cloned.1.call-done = bf16[512,1408]{1,0:T(8,128)(2,1)} async-done(((bf16[2048,1408]{1,0:T(8,128)(2,1)}), bf16[512,1408]{1,0:T(8,128)(2,1)}) %reduce-scatter.42.cloned.1.call-update) | async-done | bytes 1441808 | tf_op jit(solution)/shard_map/reduce_scatter | solution.py:320
  1125.8 65.6 %reduce-scatter.44.cloned.1.call-done = bf16[1408,512]{1,0:T(8,128)(2,1)} async-done(((bf16[1408,2048]{1,0:T(8,128)(2,1)}), bf16[1408,512]{1,0:T(8,128)(2,1)}) %reduce-scatter.44.cloned.1.call-update) | async-done | bytes 1441808 | tf_op jit(solution)/shard_map/reduce_scatter | solution.py:320
  1194.7 25.0 %reduce-scatter.30.cloned.1.call-done = bf16[128,512]{1,0:T(8,128)(2,1)} async-done(((bf16[512,512]{1,0:T(8,128)(2,1)}), bf16[128,512]{1,0:T(8,128)(2,1)}) %reduce-scatter.30.cloned.1.call-update) | async-done | bytes 131088 | tf_op jit(solution)/shard_map/reduce_scatter | solution.py:320
  1221.3 29.8 %reduce-scatter.32.cloned.1.call-done = bf16[256,512]{1,0:T(8,128)(2,1)} async-done(((bf16[256,2048]{1,0:T(8,128)(2,1)}), bf16[256,512]{1,0:T(8,128)(2,1)}) %reduce-scatter.32.cloned.1.call-update) | async-done | bytes 262160 | tf_op jit(solution)/shard_map/reduce_scatter | solution.py:320
  1253.0 32.1 %reduce-scatter.26.cloned.1.call-done = bf16[512,384]{1,0:T(8,128)(2,1)} async-done(((bf16[2048,384]{1,0:T(8,128)(2,1)}), bf16[512,384]{1,0:T(8,128)(2,1)}) %reduce-scatter.26.cloned.1.call-update) | async-done | bytes 393232 | tf_op jit(solution)/shard_map/reduce_scatter | solution.py:320
  1287.1 25.8 %reduce-scatter.28.cloned.1.call-done = bf16[64,576]{1,0:T(8,128)(2,1)} async-done(((bf16[256,576]{1,0:T(8,128)(2,1)}), bf16[64,576]{1,0:T(8,128)(2,1)}) %reduce-scatter.28.cloned.1.call-update) | async-done | bytes 73744 | tf_op jit(solution)/shard_map/reduce_scatter | solution.py:320
  1314.5 50.7 %reduce-scatter.24.cloned.1.call-done = bf16[128,2048]{1,0:T(8,128)(2,1)} async-done(((bf16[1024,2048]{1,0:T(8,128)(2,1)}), bf16[128,2048]{1,0:T(8,128)(2,1)}) %reduce-scatter.24.cloned.1.call-update) | async-done | bytes 524304 | tf_op jit(solution)/shard_map/reduce_scatter | solution.py:80
  1368.3 39.6 %all-reduce.1 = f32[32,144]{1,0:T(8,128)S(1)} all-reduce(f32[32,144]{1,0:T(8,128)S(1)} %pad_maximum_fusion.7), channel_id=13, replica_groups=mesh['shard'=4,'seq'=8] {'shard','seq'}, use_global_device_ids=true, to_apply=%region_25.26.clone | all-reduce | flops 4608 | bytes 36864
  (350 shorter events, 305.2 us)
Async XLA Ops:
  7.2 63.6 %all-gather.39.cloned.1.call-start = ((), (), s32[]{:S(2)}) async-start(), calls=%async_computation.38 | async-start | bytes 4718592 | tf_op jit(solution)/shard_map/all_gather | solution.py:76
  9.3 83.4 %all-gather.21.cloned.1.call-start = ((), (), s32[]{:S(2)}) async-start(), calls=%async_computation.15 | async-start | bytes 1966080 | tf_op jit(solution)/shard_map/all_gather | solution.py:123
  10.0 143.3 %all-gather.23.cloned.1.call-start = ((), (), s32[]{:S(2)}) async-start(), calls=%async_computation.16 | async-start | bytes 2703360 | tf_op jit(solution)/shard_map/all_gather | solution.py:144
  10.8 175.8 %all-gather.25.cloned.1.call-start = ((), (), s32[]{:S(2)}) async-start(), calls=%async_computation.17 | async-start | bytes 1310720 | tf_op jit(solution)/shard_map/all_gather | solution.py:123
  11.4 228.9 %reduce-scatter.18.cloned.1.call-start = ((), (), s32[]{:S(2)}) async-start(), calls=%async_computation.18 | async-start | bytes 4718592 | tf_op jit(solution)/shard_map/reduce_scatter | solution.py:80
  191.3 95.8 %all-gather.47.cloned.1.call-start = ((), (), s32[]{:S(2)}) async-start(), calls=%async_computation.42 | async-start | bytes 4718592 | tf_op jit(solution)/shard_map/all_gather | solution.py:76
  192.0 161.4 %all-gather.45.cloned.1.call-start = ((), (), s32[]{:S(2)}) async-start(), calls=%async_computation.41 | async-start | bytes 7208960 | tf_op jit(solution)/shard_map/all_gather | solution.py:123
  192.7 228.2 %all-gather.43.cloned.1.call-start = ((), (), s32[]{:S(2)}) async-start(), calls=%async_computation.40 | async-start | bytes 7208960 | tf_op jit(solution)/shard_map/all_gather | solution.py:123
  193.5 276.5 %all-gather.27.cloned.1.call-start = ((), (), s32[]{:S(2)}) async-start(), calls=%async_computation.19 | async-start | bytes 4718592 | tf_op jit(solution)/shard_map/all_gather | solution.py:76
  193.6 509.5 %copy-start.35 = (f32[2048]{0:T(1024)}, f32[2048]{0:T(1024)S(1)}, u32[]{:S(2)}) copy-start(f32[2048]{0:T(1024)S(1)} %mul.554) | copy-start | bytes 24580
  241.6 461.5 %copy-start.43 = (f32[128]{0:T(128)}, f32[128]{0:T(128)S(1)}, u32[]{:S(2)}) copy-start(f32[128]{0:T(128)S(1)} %get-tuple-element.262) | copy-start | bytes 1540
  241.6 461.5 %copy-start.53 = (f32[128]{0:T(128)}, f32[128]{0:T(128)S(1)}, u32[]{:S(2)}) copy-start(f32[128]{0:T(128)S(1)} %get-tuple-element.261) | copy-start | bytes 1540
  243.6 292.6 %all-gather.41.cloned.1.call-start = ((), (), s32[]{:S(2)}) async-start(), calls=%async_computation.39 | async-start | bytes 7208960 | tf_op jit(solution)/shard_map/all_gather | solution.py:123
  244.2 323.5 %all-gather.29.cloned.1.call-start = ((), (), s32[]{:S(2)}) async-start(), calls=%async_computation.20 | async-start | bytes 1802240 | tf_op jit(solution)/shard_map/all_gather | solution.py:123
  245.0 354.1 %all-gather.31.cloned.1.call-start = ((), (), s32[]{:S(2)}) async-start(), calls=%async_computation.21 | async-start | bytes 1802240 | tf_op jit(solution)/shard_map/all_gather | solution.py:123
  245.5 385.0 %all-gather.33.cloned.1.call-start = ((), (), s32[]{:S(2)}) async-start(), calls=%async_computation.22 | async-start | bytes 1802240 | tf_op jit(solution)/shard_map/all_gather | solution.py:123
  246.3 454.7 %reduce-scatter.22.cloned.1.call-start = ((), (), s32[]{:S(2)}) async-start(), calls=%async_computation.24 | async-start | bytes 4718592 | tf_op jit(solution)/shard_map/reduce_scatter | solution.py:80
  650.8 100.0 %all-gather.35.cloned.1.call-start = ((), (), s32[]{:S(2)}) async-start(), calls=%async_computation.25 | async-start | bytes 4718592 | tf_op jit(solution)/shard_map/all_gather | solution.py:76
  705.4 153.5 %reduce-scatter.46.cloned.1.call-start = ((), (), s32[]{:S(2)}) async-start(), calls=%async_computation.43 | async-start | bytes 1474560
  826.4 104.3 %all-gather.37.cloned.1.call-start = ((), (), s32[]{:S(2)}) async-start(), calls=%async_computation.28 | async-start | bytes 1327104 | tf_op jit(solution)/shard_map/all_gather | solution.py:76
  864.4 88.1 %reduce-scatter.34.cloned.1.call-start = ((), (), s32[]{:S(2)}) async-start(), calls=%async_computation.32 | async-start | bytes 1802240 | tf_op jit(solution)/shard_map/reduce_scatter | solution.py:320
  869.8 84.5 %reduce-scatter.36.cloned.1.call-start = ((), (), s32[]{:S(2)}) async-start(), calls=%async_computation.33 | async-start | bytes 1802240 | tf_op jit(solution)/shard_map/reduce_scatter | solution.py:320
  874.9 110.3 %reduce-scatter.38.cloned.1.call-start = ((), (), s32[]{:S(2)}) async-start(), calls=%async_computation.34 | async-start | bytes 1802240 | tf_op jit(solution)/shard_map/reduce_scatter | solution.py:320
  880.2 173.7 %reduce-scatter.40.cloned.1.call-start = ((), (), s32[]{:S(2)}) async-start(), calls=%async_computation.35 | async-start | bytes 7208960 | tf_op jit(solution)/shard_map/reduce_scatter | solution.py:320
  891.4 231.2 %reduce-scatter.42.cloned.1.call-start = ((), (), s32[]{:S(2)}) async-start(), calls=%async_computation.36 | async-start | bytes 7208960 | tf_op jit(solution)/shard_map/reduce_scatter | solution.py:320
  902.5 288.9 %reduce-scatter.44.cloned.1.call-start = ((), (), s32[]{:S(2)}) async-start(), calls=%async_computation.37 | async-start | bytes 7208960 | tf_op jit(solution)/shard_map/reduce_scatter | solution.py:320
  913.9 305.8 %reduce-scatter.30.cloned.1.call-start = ((), (), s32[]{:S(2)}) async-start(), calls=%async_computation.30 | async-start | bytes 655360 | tf_op jit(solution)/shard_map/reduce_scatter | solution.py:320
  917.4 333.8 %reduce-scatter.32.cloned.1.call-start = ((), (), s32[]{:S(2)}) async-start(), calls=%async_computation.31 | async-start | bytes 1310720 | tf_op jit(solution)/shard_map/reduce_scatter | solution.py:320
  922.1 363.1 %reduce-scatter.26.cloned.1.call-start = ((), (), s32[]{:S(2)}) async-start(), calls=%async_computation.27 | async-start | bytes 1966080 | tf_op jit(solution)/shard_map/reduce_scatter | solution.py:320
  929.4 383.4 %reduce-scatter.28.cloned.1.call-start = ((), (), s32[]{:S(2)}) async-start(), calls=%async_computation.29 | async-start | bytes 409600 | tf_op jit(solution)/shard_map/reduce_scatter | solution.py:320
  933.4 431.8 %reduce-scatter.24.cloned.1.call-start = ((), (), s32[]{:S(2)}) async-start(), calls=%async_computation.26 | async-start | bytes 4718592 | tf_op jit(solution)/shard_map/reduce_scatter | solution.py:80
  937.8 479.1 %reduce-scatter.20.cloned.1.call-start = ((), (), s32[]{:S(2)}) async-start(), calls=%async_computation.23 | async-start | bytes 4718592 | tf_op jit(solution)/shard_map/reduce_scatter | solution.py:80
  (65 other events, 3467.3 us)
Sparse Core Ops, SparseCore 0:
  10.1 51.5 all-gather.38
  63.6 29.0 all-gather.20
  95.6 57.7 all-gather.22
  155.1 25.1 all-gather.24
  191.4 48.7 reduce-scatter.17
  241.7 45.4 all-gather.46
  289.0 64.3 all-gather.44
  355.2 65.6 all-gather.42
  423.1 46.8 all-gather.26
  471.7 64.4 all-gather.40
  538.0 29.6 all-gather.28
  569.4 29.6 all-gather.30
  600.8 29.6 all-gather.32
  651.0 49.9 reduce-scatter.21
  705.5 45.3 all-gather.34
  826.5 32.2 reduce-scatter.45
  864.5 22.6 all-gather.36
  890.0 28.8 reduce-scatter.33
  921.8 30.2 reduce-scatter.35
  954.9 30.2 reduce-scatter.37
  988.2 65.6 reduce-scatter.39
  1056.9 65.6 reduce-scatter.41
  1125.6 65.6 reduce-scatter.43
  1194.6 25.0 reduce-scatter.29
  1223.2 27.9 reduce-scatter.31
  1254.0 31.1 reduce-scatter.25
  1288.4 24.4 reduce-scatter.27
  1315.2 49.8 reduce-scatter.23
  1367.4 49.4 reduce-scatter.19
